TPU v7x, 128 devices: a whole 4x4x4 slice. The times are simulated.
128 devices in a mesh: grp: 4 (over z), kv: 16 (over x, y), tp: 2 (over core).
Axes of the slice: x: 4, y: 4, z: 4, core: 2. Of those that a mesh axis runs over, the one named last changes fastest.
Arguments:
- hidden_states: bfloat16 [512, 4096], P('grp', 'kv'), may hold values from -6 to 6
- attn_gain: float32 [4096], P('kv'), may hold values from 0.25 to 1.75
- mlp_gain: float32 [4096], replicated, may hold values from 0.25 to 1.75
- w_query: bfloat16 [4096, 4096], P('kv', 'tp'), may hold values from -0.09375 to 0.09375
- w_out: bfloat16 [32, 128, 4096], P('tp', 'kv'), may hold values from -1 to 1
- w_gate: bfloat16 [4096, 14336], P(None, ('kv', 'tp')), may hold values from -0.09375 to 0.09375
- w_up: bfloat16 [4096, 14336], P(None, ('kv', 'tp')), may hold values from -0.09375 to 0.09375
- w_down: bfloat16 [14336, 4096], P(('kv', 'tp')), may hold values from -0.046875 to 0.046875
- kv_pool: bfloat16 [1024, 2, 128, 1024], P(('grp', 'kv'), None, None, 'tp'), may hold values from -110 to 110
- resident_cache: bfloat16 [4, 128, 2, 128, 1024], P('grp', 'kv', None, None, 'tp'), may hold values from -110 to 110
- resident_slot: int32 [4, 128], P('grp', 'kv'), may hold values from 0 to 127
- resident_len: int32 [4, 128], P('grp', 'kv'), may hold values from 1 to 128
- new_owner: int32 [4, 256], replicated, may hold values from 0 to 63, as said below
- new_local: int32 [4, 256], replicated, may hold values from 0 to 15
- new_slot: int32 [4, 256], P('grp', 'kv'), may hold values from 0 to 127
- new_len: int32 [4, 256], P('grp', 'kv'), may hold values from 1 to 128
- token_kv: bfloat16 [512, 2, 1024], P('grp', None, 'tp'), may hold values from -6 to 6
Outputs:
- mixed: bfloat16 [512, 4096], P(('grp', 'kv', 'tp'))
- new_cache: bfloat16 [4, 256, 2, 128, 1024], P('grp', 'kv', None, None, 'tp')
Inputs may be any that keep to these rules, and one draw needn't show every extreme that they name: New page c of group g is kept by the device of kv index c // 16 of group g and comes from the device whose index along grp+kv is new_owner[g, c]; every decode device receives exactly 4 new pages from the owners of each grp index; no owner sends more than 1 pages to the devices of one kv index over all groups, so at most 1 to one device; every owner sends each of its 16 pages exactly once.
All inputs are finite; a program needn't handle non-finite values.
Results may differ from a plain program's by a relative error of at most 0.018.
Values may be sent and summed in bfloat16 or wider, within the bound.
A program may use at most 128 MiB of HBM per device.

v0:
```python
import jax
import jax.numpy as jnp
from jax import lax
from jax.sharding import Mesh
from jax.sharding import PartitionSpec as P

D = 4096
HEADS = 32
KV_HEADS = 8
HEAD_DIM = 128
NPR = 4
KV = ("kv_0", "kv_1")
KV_TP = ("kv_0", "kv_1", "tp")
GRP_KV = ("grp", "kv_0", "kv_1")
GRP_KV_TP = ("grp", "kv_0", "kv_1", "tp")
neg_fill = -1e30
norm_eps = 1e-05


def combined_by_axis(shard, axes, combine):
    for axis in axes:
        pieces = jax.tree.map(lambda part: lax.all_gather(part, axis), shard)
        shard = jax.tree.map(lambda part: part[0], pieces)
        for k in range(1, lax.axis_size(axis)):
            shard = combine(shard, jax.tree.map(lambda part: part[k], pieces))
    return shard


def split_up(shard, dim, peers):
    before, after = (shard.shape[:dim], shard.shape[dim + 1 :])
    return jnp.moveaxis(shard.reshape(*before, peers, -1, *after), dim, 0)


def summed_on_arrival(shard, axis, dim):
    tiles = split_up(shard, dim, lax.axis_size(axis))
    arrived = lax.all_to_all(tiles, axis, split_axis=0, concat_axis=0, tiled=True)
    return arrived.astype(jnp.float32).sum(axis=0)


def combine(earlier, later):
    top_a, sum_a, acc_a = earlier
    top_b, sum_b, acc_b = later
    top = jnp.maximum(top_a, top_b)
    fade_a = jnp.exp(top_a - top)
    fade_b = jnp.exp(top_b - top)
    return (
        top,
        sum_a * fade_a + sum_b * fade_b,
        acc_a * fade_a[..., None] + acc_b * fade_b[..., None],
    )


def nth_match(table, wanted, places):
    matched = (table == wanted).astype(jnp.int32)
    ranking = jnp.cumsum(matched, axis=1) - 1
    return (matched[:, None, :] == 1) & (ranking[:, None, :] == places[None, :, None])


def move_pages(kv_pool, new_owner, new_local):
    groups = lax.axis_size("grp")
    ranks = lax.axis_size(KV)
    per_dev = new_owner.shape[1] // ranks
    cap = groups * NPR // ranks
    grp_rank = lax.axis_index("grp")
    kv_rank = lax.axis_index(KV)
    owners = new_owner.reshape(groups * ranks, per_dev)
    myself = grp_rank * ranks + kv_rank
    places = jnp.arange(cap, dtype=jnp.int32)
    mine = lax.dynamic_index_in_dim(owners, myself, 0, keepdims=False)
    order = jnp.arange(per_dev, dtype=jnp.int32)
    by_col = (
        new_owner.reshape(groups, ranks, per_dev)
        .transpose(1, 0, 2)
        .reshape(ranks, groups * per_dev)
    )
    local_col = (
        new_local.reshape(groups, ranks, per_dev)
        .transpose(1, 0, 2)
        .reshape(ranks, groups * per_dev)
    )
    select = nth_match(by_col, myself, places)
    picked = jnp.sum(jnp.where(select, local_col[:, None, :], 0), axis=2)
    outgoing = jnp.take(kv_pool, picked.reshape(-1), axis=0)
    received = lax.all_to_all(outgoing, KV, split_axis=0, concat_axis=0, tiled=True)
    row_here = lax.dynamic_index_in_dim(by_col, kv_rank, 0, keepdims=False)
    sources = grp_rank * ranks + jnp.arange(ranks, dtype=jnp.int32)
    hits = nth_match(
        jnp.broadcast_to(row_here[None, :], (ranks, row_here.shape[0])), sources[:, None], places
    )
    spots = jnp.arange(row_here.shape[0], dtype=jnp.int32)
    where_f = jnp.sum(jnp.where(hits, spots[None, None, :], 0), axis=2).reshape(-1)
    dest_grp = where_f // per_dev
    dest_pos = where_f % per_dev
    same = (dest_grp[:, None] == dest_grp[None, :]) & (dest_pos[:, None] < dest_pos[None, :])
    rank_in = jnp.sum(same.astype(jnp.int32), axis=0)
    target = dest_grp * NPR + rank_in
    items = jnp.arange(target.shape[0], dtype=jnp.int32)
    inverse = jnp.sum(jnp.where(target[None, :] == items[:, None], items[None, :], 0), axis=1)
    sorted_pages = jnp.take(received, inverse, axis=0)
    arrived = lax.all_to_all(sorted_pages, "grp", split_axis=0, concat_axis=0, tiled=True)
    src_grp = mine // ranks
    earlier = (src_grp[:, None] == src_grp[None, :]) & (order[:, None] < order[None, :])
    before = jnp.sum(earlier.astype(jnp.int32), axis=0)
    return jnp.take(arrived, src_grp * NPR + before, axis=0)


def local_partials(query, resident, arrived, res_slot, res_len, arr_slot, arr_len, token_kv, first):
    pages = jnp.concatenate([resident, arrived], axis=0)
    owner_slot = jnp.concatenate([res_slot, arr_slot])
    filled = jnp.concatenate([res_len, arr_len])
    count = pages.shape[0]
    tokens = pages.shape[2]
    kv_here = pages.shape[3] // HEAD_DIM
    slots = query.shape[0]
    ratio = HEADS // KV_HEADS
    keys = pages[:, 0].astype(jnp.float32).reshape(count, tokens, kv_here, HEAD_DIM)
    values = pages[:, 1].astype(jnp.float32).reshape(count, tokens, kv_here, HEAD_DIM)
    grouped = query.reshape(slots, kv_here, ratio, HEAD_DIM)
    picked = jnp.take(grouped, owner_slot, axis=0)
    scores = jnp.einsum("ikgd,itkd->ikgt", picked, keys, precision=lax.Precision.HIGHEST)
    usable = (jnp.arange(tokens, dtype=jnp.int32)[None, :] < filled[:, None])[:, None, None, :]
    scores = jnp.where(usable, scores, neg_fill)
    page_top = jnp.max(scores, axis=3)
    member = owner_slot[None, :] == jnp.arange(slots, dtype=jnp.int32)[:, None]
    slot_top = jnp.max(jnp.where(member[:, :, None, None], page_top[None], neg_fill), axis=1)
    own_keys = token_kv[:, 0].astype(jnp.float32).reshape(slots, kv_here, HEAD_DIM)
    own_values = token_kv[:, 1].astype(jnp.float32).reshape(slots, kv_here, HEAD_DIM)
    own_score = jnp.einsum("skgd,skd->skg", grouped, own_keys, precision=lax.Precision.HIGHEST)
    own_score = jnp.where(first, own_score, neg_fill)
    slot_top = jnp.maximum(slot_top, own_score)
    reach = jnp.take(slot_top, owner_slot, axis=0)
    weights = jnp.where(usable, jnp.exp(scores - reach[..., None]), 0.0)
    page_sum = jnp.sum(weights, axis=3)
    page_acc = jnp.einsum("ikgt,itkd->ikgd", weights, values, precision=lax.Precision.HIGHEST)
    own_weight = jnp.where(first, jnp.exp(own_score - slot_top), 0.0)
    member_f = member.astype(jnp.float32)
    total = jnp.dot(member_f, page_sum.reshape(count, -1), precision=lax.Precision.HIGHEST)
    total = total + own_weight.reshape(slots, -1)
    weighted = jnp.dot(member_f, page_acc.reshape(count, -1), precision=lax.Precision.HIGHEST)
    weighted = (
        weighted.reshape(slots, kv_here, ratio, HEAD_DIM)
        + own_weight[..., None] * own_values[:, :, None, :]
    )
    return (slot_top.reshape(slots, -1), total, weighted.reshape(slots, kv_here * ratio, HEAD_DIM))


def per_device(
    hidden_states,
    attn_gain,
    mlp_gain,
    w_query,
    w_out,
    w_gate,
    w_up,
    w_down,
    kv_pool,
    resident_cache,
    resident_slot,
    resident_len,
    new_owner,
    new_local,
    new_slot,
    new_len,
    token_kv,
):
    ranks = lax.axis_size(KV)
    pairs = lax.axis_size("tp")
    kv_rank = lax.axis_index(KV)
    tp_rank = lax.axis_index("tp")
    features = hidden_states.astype(jnp.float32)
    partial_query = jnp.dot(
        (features * attn_gain).astype(jnp.bfloat16), w_query, preferred_element_type=jnp.float32
    )
    squares = jnp.sum(features * features, axis=1)
    partial_query, squares = lax.psum((partial_query, squares), KV)
    attn_scale = lax.rsqrt(squares / D + norm_eps)
    query = partial_query * attn_scale[:, None] * HEAD_DIM ** (-0.5)
    new_pages = move_pages(kv_pool, new_owner, new_local)
    top, total, weighted = local_partials(
        query,
        resident_cache[0],
        new_pages,
        resident_slot[0],
        resident_len[0],
        new_slot[0],
        new_len[0],
        token_kv,
        kv_rank == 0,
    )
    top, total, weighted = combined_by_axis((top, total, weighted), KV, combine)
    attn = (weighted / total[..., None]).astype(jnp.bfloat16)
    slots = attn.shape[0]
    heads_here = attn.shape[1]
    span = HEAD_DIM // ranks
    piece = lax.dynamic_slice_in_dim(attn, kv_rank * span, span, 2)
    branch = jnp.dot(
        piece.reshape(slots, heads_here * span),
        w_out.reshape(heads_here * span, w_out.shape[2]),
        preferred_element_type=jnp.float32,
    )
    width_here = hidden_states.shape[1]
    laid = branch.reshape(slots, ranks, width_here)
    spot = (jnp.arange(ranks, dtype=jnp.int32) == kv_rank) & (tp_rank == 0)
    laid = laid + jnp.where(spot[None, :, None], features[:, None, :], 0.0)
    resid = lax.psum(laid.reshape(slots, ranks * width_here).astype(jnp.bfloat16), KV_TP)
    resid_f = resid.astype(jnp.float32)
    mlp_scale = lax.rsqrt(jnp.sum(resid_f * resid_f, axis=1) / D + norm_eps)
    normed_mlp = (resid_f * mlp_gain).astype(jnp.bfloat16)
    gate = jnp.dot(normed_mlp, w_gate, preferred_element_type=jnp.float32) * mlp_scale[:, None]
    upward = jnp.dot(normed_mlp, w_up, preferred_element_type=jnp.float32) * mlp_scale[:, None]
    hidden_units = (jax.nn.silu(gate) * upward).astype(jnp.bfloat16)
    row_count = slots // (ranks * pairs)
    down = summed_on_arrival(
        jnp.dot(hidden_units, w_down, preferred_element_type=jnp.float32).astype(jnp.bfloat16),
        KV_TP,
        0,
    )
    row_start = (kv_rank * pairs + tp_rank) * row_count
    kept = lax.dynamic_slice_in_dim(resid_f, row_start, row_count, 0)
    mixed = (kept + down).astype(jnp.bfloat16)
    return (mixed, new_pages[None])


def solution(mesh):
    finer = Mesh(
        mesh.devices.reshape(mesh.shape["grp"], 4, 4, mesh.shape["tp"]),
        ("grp", "kv_0", "kv_1", "tp"),
    )
    return jax.shard_map(
        per_device,
        mesh=finer,
        in_specs=(
            P("grp", KV),
            P(KV),
            P(),
            P(KV, "tp"),
            P("tp", KV, None),
            P(None, KV_TP),
            P(None, KV_TP),
            P(KV_TP, None),
            P(GRP_KV, None, None, "tp"),
            P("grp", KV, None, None, "tp"),
            P("grp", KV),
            P("grp", KV),
            P(),
            P(),
            P("grp", KV),
            P("grp", KV),
            P("grp", None, "tp"),
        ),
        out_specs=(P(GRP_KV_TP, None), P("grp", KV, None, None, "tp")),
        check_vma=False,
    )
```

profile of v0, /device:TPU:1, one launch (start us, length us, event | category | flops | bytes accessed | tf_op | source)
XLA Modules:
  0.0 507.7 jit_solution(3619202428460434715)
XLA Ops:
  7.2 0.9 reshape.659
  8.0 0.8 reshape.662
  8.9 0.2 reduce_window_sum.17
  9.2 0.8 reshape.661
  10.0 0.4 fusion.34
  10.4 5.0 gather_fusion.2
  15.5 4.7 broadcast_select_fusion.2
  20.1 7.6 %all-to-all-start = ((bf16[16,2,128,512]{3,2,1,0:T(8,128)(2,1)}), bf16[16,2,128,512]{3,2,1,0:T(8,128)(2,1)}, u32[]{:S(2)}, u32[]{:S(2)}) async-start(bf16[16,2,128,512]{3,2,1,0:T(8,128)(2,1)} %broadcast_select_fusion.2), calls=%async_computation | async-start | bytes 8388608 | tf_op jit(solution)/shard_map/all_to_all | solution.py:84
  27.9 0.2 reduce_window_sum.18
  28.1 0.2 select_reduce_fusion.2
  28.5 59.5 %all-to-all-done = bf16[16,2,128,512]{3,2,1,0:T(8,128)(2,1)} async-done(((bf16[16,2,128,512]{3,2,1,0:T(8,128)(2,1)}), bf16[16,2,128,512]{3,2,1,0:T(8,128)(2,1)}, u32[]{:S(2)}, u32[]{:S(2)}) %all-to-all-start) | async-done | bytes 4194336 | tf_op jit(solution)/shard_map/all_to_all | solution.py:84
  88.1 5.0 gather_fusion.3
  93.1 4.7 broadcast_select_fusion.1
  97.8 5.2 %all-to-all-start.1 = ((bf16[16,2,128,512]{3,2,1,0:T(8,128)(2,1)}), bf16[16,2,128,512]{3,2,1,0:T(8,128)(2,1)}, u32[]{:S(2)}, u32[]{:S(2)}) async-start(bf16[16,2,128,512]{3,2,1,0:T(8,128)(2,1)} %broadcast_select_fusion.1), calls=%async_computation.1 | async-start | bytes 8388608 | tf_op jit(solution)/shard_map/all_to_all | solution.py:100
  103.0 1.3 fusion.25
  104.8 0.4 fusion.79
  105.2 0.2 copy.185
  105.4 0.2 copy.179
  105.6 33.9 %psum.22 = f32[128]{0:T(128)S(1)} all-reduce(f32[128]{0:T(128)S(1)} %multiply_reduce_fusion.1), channel_id=1, replica_groups=mesh['grp'=4,'kv_0'=4,'kv_1'=4,'tp'=2] {'kv_0','kv_1'}, use_global_device_ids=true, to_apply=%region_2.0 | all-reduce | flops 128 | bytes 1024 | tf_op jit(solution)/shard_map/psum | solution.py:175
  139.8 61.1 %all-reduce.3.cloned.1.call-done = f32[128,2048]{1,0:T(8,128)} async-done(((f32[128,2048]{1,0:T(8,128)}), f32[128,2048]{1,0:T(8,128)}) %all-reduce.3.cloned.1.call-update) | async-done | bytes 1048592 | tf_op jit(solution)/shard_map/psum | solution.py:175
  200.9 1.4 multiply_multiply_fusion
  202.3 0.7 reshape.658
  203.0 0.7 gather_fusion
  203.7 1.8 fusion.81
  205.5 5.0 gather_fusion.4
  210.6 2.8 broadcast_select_fusion
  213.4 2.9 pad_maximum_fusion
  216.3 4.7 copy.150
  221.0 4.6 fusion.80
  226.2 0.6 gather_fusion.1
  227.0 4.7 copy.155
  231.7 6.9 %fusion.17 = f32[24,4,4,128]{3,2,1,0:T(4,128)S(1)} fusion(bf16[24,128,4,128]{1,3,2,0:T(8,128)(2,1)} %bitcast.217, f32[24,4,4,128]{3,2,1,0:T(4,128)S(1)} %get-tuple-element.40, f32[24,4,4]{2,1,0:T(4,128)S(1)} %broadcast_select_fusion.3, pred[24,128]{1,0:T(8,128)(4,1)S(1)} %iota_compare_fusion), kind=kOutput, calls=%fused_computation.52 | convolution fusion | flops 75595776 | bytes 3543552 | tf_op jit(solution)/shard_map/ikgt,itkd->ikgd/dot_general | solution.py:134
  238.9 0.7 convolution_add_fusion
  239.6 1.6 copy.160
  241.4 9.3 %all_gather.25 = f32[4,128,16]{1,2,0:T(8,128)S(1)} all-gather(f32[1,128,16]{1,2,0:T(8,128)S(1)} %bitcast.229), channel_id=1, replica_groups=mesh['grp'=4,'kv_0'=4,'kv_1'=4,'tp'=2] {'kv_0'}, dimensions={0}, use_global_device_ids=true | all-gather | bytes 40960 | tf_op jit(solution)/shard_map/all_gather | solution.py:22
  251.3 38.9 %all-gather.4.cloned.1.call-done = f32[4,128,16,128]{3,2,1,0:T(8,128)} async-done(((f32[1,128,16,128]{3,2,1,0:T(8,128)}), f32[4,128,16,128]{3,2,1,0:T(8,128)}) %all-gather.4.cloned.1.call-update) | async-done | bytes 4194320 | tf_op jit(solution)/shard_map/all_gather | solution.py:22
  290.2 4.8 fusion.3
  295.1 1.3 copy.174
  296.4 0.4 fusion.16
  296.9 0.2 convolution_add_fusion.1
  297.1 9.0 %all-gather = f32[512,16]{0,1:T(8,128)S(1)} all-gather(f32[128,16]{0,1:T(8,128)S(1)} %convolution_add_fusion.1), channel_id=2, replica_groups=mesh['grp'=4,'kv_0'=4,'kv_1'=4,'tp'=2] {'kv_0'}, dimensions={0}, use_global_device_ids=true | all-gather | bytes 40960 | tf_op jit(solution)/shard_map/all_gather | solution.py:22
  306.2 10.8 %all_gather.27 = f32[4,128,16]{1,2,0:T(8,128)S(1)} all-gather(f32[1,128,16]{1,2,0:T(8,128)S(1)} %get-tuple-element.15), channel_id=1, replica_groups=mesh['grp'=4,'kv_0'=4,'kv_1'=4,'tp'=2] {'kv_1'}, dimensions={0}, use_global_device_ids=true | all-gather | bytes 40960 | tf_op jit(solution)/shard_map/all_gather | solution.py:22
  317.0 10.6 %all_gather.30 = f32[4,128,16]{1,2,0:T(8,128)S(1)} all-gather(f32[1,128,16]{1,2,0:T(8,128)S(1)} %get-tuple-element.14), channel_id=1, replica_groups=mesh['grp'=4,'kv_0'=4,'kv_1'=4,'tp'=2] {'kv_1'}, dimensions={0}, use_global_device_ids=true | all-gather | bytes 40960 | tf_op jit(solution)/shard_map/all_gather | solution.py:22
  327.6 16.7 %all-gather.6.cloned.1.call-done = f32[4,128,16,128]{3,2,1,0:T(8,128)} async-done(((f32[1,128,16,128]{3,2,1,0:T(8,128)}), f32[4,128,16,128]{3,2,1,0:T(8,128)}) %all-gather.6.cloned.1.call-update) | async-done | bytes 4194320 | tf_op jit(solution)/shard_map/all_gather | solution.py:22
  344.3 3.9 fusion.78
  348.2 0.4 copy.186
  348.6 1.6 copy.187
  350.2 2.6 copy.188
  352.7 1.5 copy.189
  354.2 0.2 fusion.8
  354.4 1.8 add_convert_fusion
  356.2 0.7 copy.176
  356.9 1.4 copy.177
  358.2 105.7 %all-reduce.5.cloned.1.call-done = bf16[128,4096]{1,0:T(8,128)(2,1)} async-done(((bf16[128,4096]{1,0:T(8,128)(2,1)}), bf16[128,4096]{1,0:T(8,128)(2,1)}) %all-reduce.5.cloned.1.call-update) | async-done | bytes 1048592 | tf_op jit(solution)/shard_map/psum | solution.py:205
  463.9 1.6 multiply_reduce_fusion
  465.5 3.5 convolution_multiply_fusion.1
  469.0 6.0 %convolution_convert_fusion = bf16[128,4096]{1,0:T(8,128)(2,1)S(1)} fusion(bf16[448,4096]{1,0:T(8,128)(2,1)} %param.26, bf16[4096,448]{0,1:T(8,128)(2,1)} %param.25, f32[4096]{0:T(1024)S(1)} %copy-done.7, bf16[128,4096]{1,0:T(8,128)(2,1)S(1)} %copy-done.2, f32[128,448]{0,1:T(8,128)S(1)} %convolution_multiply_fusion.1, f32[128]{0:T(128)S(1)} %add_rsqrt_fusion), kind=kOutput, calls=%fused_computation.7 | convolution fusion | flops 942022656 | bytes 9683456 | tf_op jit(solution)/shard_map/dot_general | solution.py:214
  475.0 1.2 reshape.671
  476.3 6.1 %all-to-all-start.2 = ((bf16[32,4,4096]{2,1,0:T(4,128)(2,1)}), bf16[32,4,4096]{2,1,0:T(4,128)(2,1)S(1)}, u32[]{:S(2)}, u32[]{:S(2)}) async-start(bf16[32,4,4096]{2,1,0:T(4,128)(2,1)} %reshape.671), calls=%async_computation.2 | async-start | bytes 2097152 | tf_op jit(solution)/shard_map/all_to_all | solution.py:36
  482.3 4.8 fusion.92
  487.1 1.6 convert_element_type.85
  488.7 10.6 %all-to-all-done.2 = bf16[32,4,4096]{2,1,0:T(4,128)(2,1)S(1)} async-done(((bf16[32,4,4096]{2,1,0:T(4,128)(2,1)}), bf16[32,4,4096]{2,1,0:T(4,128)(2,1)S(1)}, u32[]{:S(2)}, u32[]{:S(2)}) %all-to-all-start.2) | async-done | bytes 1048608 | tf_op jit(solution)/shard_map/all_to_all | solution.py:36
  499.2 0.4 convert_reduce_fusion
  499.7 1.5 add_convert_fusion.1
  (89 shorter events, 3.4 us)
Async XLA Ops:
  7.2 95.8 %copy-start = (bf16[256,2048]{1,0:T(8,128)(2,1)S(1)}, bf16[256,2048]{1,0:T(8,128)(2,1)}, u32[]{:S(2)}) copy-start(bf16[256,2048]{1,0:T(8,128)(2,1)} %param.22) | copy-start | bytes 3145732
  20.1 68.0 %all-to-all-start = ((bf16[16,2,128,512]{3,2,1,0:T(8,128)(2,1)}), bf16[16,2,128,512]{3,2,1,0:T(8,128)(2,1)}, u32[]{:S(2)}, u32[]{:S(2)}) async-start(bf16[16,2,128,512]{3,2,1,0:T(8,128)(2,1)} %broadcast_select_fusion.2), calls=%async_computation | async-start | bytes 8388608 | tf_op jit(solution)/shard_map/all_to_all | solution.py:84
  97.8 5.3 %copy-start.6 = (bf16[128,256]{1,0:T(8,128)(2,1)S(1)}, bf16[128,256]{1,0:T(8,128)(2,1)}, u32[]{:S(2)}) copy-start(bf16[128,256]{1,0:T(8,128)(2,1)} %param.19) | copy-start | bytes 196612
  97.8 5.3 %copy-start.8 = (f32[256]{0:T(256)S(1)}, f32[256]{0:T(256)}, u32[]{:S(2)}) copy-start(f32[256]{0:T(256)} %param.20) | copy-start | bytes 3076
  97.8 6.7 %copy-start.9 = (s32[1,16]{1,0:T(1,128)S(1)}, s32[1,16]{1,0:T(1,128)}, u32[]{:S(2)}) copy-start(s32[1,16]{1,0:T(1,128)} %param.33) | copy-start | bytes 196
  97.8 6.7 %copy-start.10 = (s32[1,8]{1,0:T(1,128)S(1)}, s32[1,8]{1,0:T(1,128)}, u32[]{:S(2)}) copy-start(s32[1,8]{1,0:T(1,128)} %param.29) | copy-start | bytes 100
  97.8 7.0 %copy-start.5 = (bf16[128,2,512]{2,1,0:T(2,128)(2,1)S(1)}, bf16[128,2,512]{2,1,0:T(2,128)(2,1)}, u32[]{:S(2)}) copy-start(bf16[128,2,512]{2,1,0:T(2,128)(2,1)} %param.35) | copy-start | bytes 786436
  97.8 107.8 %all-to-all-start.1 = ((bf16[16,2,128,512]{3,2,1,0:T(8,128)(2,1)}), bf16[16,2,128,512]{3,2,1,0:T(8,128)(2,1)}, u32[]{:S(2)}, u32[]{:S(2)}) async-start(bf16[16,2,128,512]{3,2,1,0:T(8,128)(2,1)} %broadcast_select_fusion.1), calls=%async_computation.1 | async-start | bytes 8388608 | tf_op jit(solution)/shard_map/all_to_all | solution.py:100
  103.0 2.2 copy-start.11
  103.0 2.2 copy-start.12
  103.0 98.0 %all-reduce.3.cloned.1.call-start = ((), (), s32[]{:S(2)}) async-start(), calls=%async_computation.3 | async-start | bytes 2097152 | tf_op jit(solution)/shard_map/psum | solution.py:175
  104.4 185.8 %all-gather.4.cloned.1.call-start = ((), (), s32[]{:S(2)}) async-start(), calls=%async_computation.4 | async-start | bytes 5242880 | tf_op jit(solution)/shard_map/all_gather | solution.py:22
  210.6 2.9 copy-start.3
  241.2 103.0 %all-gather.6.cloned.1.call-start = ((), (), s32[]{:S(2)}) async-start(), calls=%async_computation.5 | async-start | bytes 5242880 | tf_op jit(solution)/shard_map/all_gather | solution.py:22
  250.7 44.4 %copy-start.4 = (bf16[16,8,4096]{2,1,0:T(8,128)(2,1)S(1)}, bf16[16,8,4096]{2,1,0:T(8,128)(2,1)}, u32[]{:S(2)}) copy-start(bf16[16,8,4096]{2,1,0:T(8,128)(2,1)} %param.23) | copy-start | bytes 3145732
  295.0 168.9 %all-reduce.5.cloned.1.call-start = ((), (), s32[]{:S(2)}) async-start(), calls=%async_computation.6 | async-start | bytes 2097152 | tf_op jit(solution)/shard_map/psum | solution.py:205
  356.2 109.3 %copy-start.7 = (f32[4096]{0:T(1024)S(1)}, f32[4096]{0:T(1024)}, u32[]{:S(2)}) copy-start(f32[4096]{0:T(1024)} %param.21) | copy-start | bytes 49156
  463.9 5.1 %copy-start.2 = (bf16[128,4096]{1,0:T(8,128)(2,1)S(1)}, bf16[128,4096]{1,0:T(8,128)(2,1)}, u32[]{:S(2)}) copy-start(bf16[128,4096]{1,0:T(8,128)(2,1)} %all-reduce.5.cloned.1.call-done) | copy-start | bytes 3145732
  476.3 23.0 %all-to-all-start.2 = ((bf16[32,4,4096]{2,1,0:T(4,128)(2,1)}), bf16[32,4,4096]{2,1,0:T(4,128)(2,1)S(1)}, u32[]{:S(2)}, u32[]{:S(2)}) async-start(bf16[32,4,4096]{2,1,0:T(4,128)(2,1)} %reshape.671), calls=%async_computation.2 | async-start | bytes 2097152 | tf_op jit(solution)/shard_map/all_to_all | solution.py:36
  482.3 18.9 %copy-start.1 = (bf16[256,2048]{1,0:T(8,128)(2,1)S(1)}, bf16[256,2048]{1,0:T(8,128)(2,1)}, u32[]{:S(2)}) copy-start(bf16[256,2048]{1,0:T(8,128)(2,1)} %param.22) | copy-start | bytes 3145732
Sparse Core Ops, SparseCore 0:
  107.0 93.8 all-reduce.2
  241.4 48.7 all-gather.3
  295.1 49.0 all-gather.5
  358.4 105.4 all-reduce.4
where the time goes:
time: 509 us; the launch traced here: 508 us
  waiting for transfers between devices  292 us (57%)
  blocking collectives  73.6 us (14%)
  local copies, waits for them, and re-layouts  47 us (9%)
  other arithmetic  34.5 us (7%)
  matrix products  26.8 us (5%)
  starting transfers between devices  19 us (4%)
  between operations  14.2 us (3%)
    psum x1, waiting for transfers between devices, per_device(): lax.psum(laid.reshape(slots, ranks * width_here).astype(jnp.bfloat16), KV...  106 us
    psum x1, waiting for transfers between devices, per_device(): partial_query, squares = lax.psum((partial_query, squares), KV)  61.1 us
    all_to_all x1, waiting for transfers between devices, move_pages(): lax.all_to_all(outgoing, KV, split_axis=0, concat_axis=0, tiled=True)  59.5 us
    all_gather x2, waiting for transfers between devices, combined_by_axis(): pieces = jax.tree.map(lambda part: lax.all_gather(part, axis), shard)  55.5 us
    all_gather x4, blocking collectives, combined_by_axis(): pieces = jax.tree.map(lambda part: lax.all_gather(part, axis), shard)  39.7 us
    psum x1, blocking collectives, per_device(): partial_query, squares = lax.psum((partial_query, squares), KV)  33.9 us
    all_to_all x1, waiting for transfers between devices, summed_on_arrival(): lax.all_to_all(tiles, axis, split_axis=0, concat_axis=0, tiled=True)  10.6 us
  transfers between devices with their start and end apart: 7, of which 6 were waited for; matrix products, arithmetic and copies ran while one was open for 3% of the time, Pallas kernels for 0%

commit v1 on v0

--- a/solution.py
+++ b/solution.py
@@ -15,6 +15,11 @@
 GRP_KV_TP = ("grp", "kv_0", "kv_1", "tp")
 neg_fill = -1e30
 norm_eps = 1e-05
+
+
+def add_all(x, name):
+    parts = lax.all_gather(x, name)
+    return jnp.sum(parts, axis=0)
 
 
 def combined_by_axis(shard, axes, combine):
@@ -202,7 +207,7 @@
     laid = branch.reshape(slots, ranks, width_here)
     spot = (jnp.arange(ranks, dtype=jnp.int32) == kv_rank) & (tp_rank == 0)
     laid = laid + jnp.where(spot[None, :, None], features[:, None, :], 0.0)
-    resid = lax.psum(laid.reshape(slots, ranks * width_here).astype(jnp.bfloat16), KV_TP)
+    resid = add_all(laid.reshape(slots, ranks * width_here).astype(jnp.bfloat16), KV_TP)
     resid_f = resid.astype(jnp.float32)
     mlp_scale = lax.rsqrt(jnp.sum(resid_f * resid_f, axis=1) / D + norm_eps)
     normed_mlp = (resid_f * mlp_gain).astype(jnp.bfloat16)

time: 509 us -> 535 us (1.051)
  other arithmetic: 34.5 us -> 46.3 us
  waiting for transfers between devices: 292 us -> 303 us
    all_gather x0 -> x1, waiting for transfers between devices: none -> 115 us  [add_all(): parts = lax.all_gather(x, name)]
    psum x1 -> x0, waiting for transfers between devices: 106 us -> none  [per_device(): lax.psum(laid.reshape(slots, ranks * width_here).astype(jnp.bfloat16), KV...]
    reduce_sum x0 -> x1, other arithmetic: none -> 11.4 us  [add_all(): return jnp.sum(parts, axis=0)]
where the time goes in v1:
time: 535 us; the launch traced here: 534 us
  waiting for transfers between devices  303 us (57%)
  blocking collectives  73.6 us (14%)
  local copies, waits for them, and re-layouts  51.9 us (10%)
  other arithmetic  46.3 us (9%)
  matrix products  26.7 us (5%)
  starting transfers between devices  18.2 us (3%)
  between operations  14.2 us (3%)
    all_gather x1, waiting for transfers between devices, add_all(): parts = lax.all_gather(x, name)  115 us
    psum x1, waiting for transfers between devices, per_device(): partial_query, squares = lax.psum((partial_query, squares), KV)  61.2 us
    all_to_all x1, waiting for transfers between devices, move_pages(): lax.all_to_all(outgoing, KV, split_axis=0, concat_axis=0, tiled=True)  59.5 us
    all_gather x2, waiting for transfers between devices, combined_by_axis(): pieces = jax.tree.map(lambda part: lax.all_gather(part, axis), shard)  55.5 us
    all_gather x4, blocking collectives, combined_by_axis(): pieces = jax.tree.map(lambda part: lax.all_gather(part, axis), shard)  39.7 us
    psum x1, blocking collectives, per_device(): partial_query, squares = lax.psum((partial_query, squares), KV)  33.8 us
    all_to_all x1, waiting for transfers between devices, summed_on_arrival(): lax.all_to_all(tiles, axis, split_axis=0, concat_axis=0, tiled=True)  12.1 us
    reduce_sum x1, other arithmetic, add_all(): return jnp.sum(parts, axis=0)  11.4 us
  transfers between devices with their start and end apart: 7, of which 6 were waited for; matrix products, arithmetic and copies ran while one was open for 3% of the time, Pallas kernels for 0%

profile of v1, /device:TPU:1, one launch (start us, length us, event | category | flops | bytes accessed | tf_op | source)
XLA Modules:
  0.0 533.9 jit_solution(9298590138253661782)
XLA Ops:
  7.2 0.9 reshape.672
  8.0 0.8 reshape.669
  8.9 0.2 reduce_window_sum.17
  9.2 0.8 reshape.671
  10.0 0.4 fusion.34
  10.4 5.0 gather_fusion.2
  15.5 4.7 broadcast_select_fusion.2
  20.1 7.6 %all-to-all-start = ((bf16[16,2,128,512]{3,2,1,0:T(8,128)(2,1)}), bf16[16,2,128,512]{3,2,1,0:T(8,128)(2,1)}, u32[]{:S(2)}, u32[]{:S(2)}) async-start(bf16[16,2,128,512]{3,2,1,0:T(8,128)(2,1)} %broadcast_select_fusion.2), calls=%async_computation | async-start | bytes 8388608 | tf_op jit(solution)/shard_map/all_to_all | solution.py:89
  27.9 0.2 reduce_window_sum.18
  28.1 0.2 select_reduce_fusion.2
  28.5 59.5 %all-to-all-done = bf16[16,2,128,512]{3,2,1,0:T(8,128)(2,1)} async-done(((bf16[16,2,128,512]{3,2,1,0:T(8,128)(2,1)}), bf16[16,2,128,512]{3,2,1,0:T(8,128)(2,1)}, u32[]{:S(2)}, u32[]{:S(2)}) %all-to-all-start) | async-done | bytes 4194336 | tf_op jit(solution)/shard_map/all_to_all | solution.py:89
  88.1 5.0 gather_fusion.3
  93.1 4.7 broadcast_select_fusion.1
  97.8 5.2 all-to-all-start.1
  103.0 1.3 fusion.25
  104.9 0.4 fusion.79
  105.7 33.8 %psum.15 = f32[128]{0:T(128)S(1)} all-reduce(f32[128]{0:T(128)S(1)} %multiply_reduce_fusion.1), channel_id=1, replica_groups=mesh['grp'=4,'kv_0'=4,'kv_1'=4,'tp'=2] {'kv_0','kv_1'}, use_global_device_ids=true, to_apply=%region_2.0 | all-reduce | flops 128 | bytes 1024 | tf_op jit(solution)/shard_map/psum | solution.py:180
  139.7 61.2 %all-reduce.2.cloned.1.call-done = f32[128,2048]{1,0:T(8,128)} async-done(((f32[128,2048]{1,0:T(8,128)}), f32[128,2048]{1,0:T(8,128)}) %all-reduce.2.cloned.1.call-update) | async-done | bytes 1048592 | tf_op jit(solution)/shard_map/psum | solution.py:180
  200.9 1.4 multiply_multiply_fusion
  202.3 0.7 reshape.668
  203.0 0.7 gather_fusion
  203.7 1.8 fusion.81
  205.5 5.0 gather_fusion.4
  210.6 2.8 broadcast_select_fusion
  213.4 3.0 pad_maximum_fusion
  216.4 4.6 copy.192
  221.0 4.7 copy.187
  225.8 4.6 fusion.80
  231.1 0.6 gather_fusion.1
  231.8 6.9 %fusion.17 = f32[24,4,4,128]{3,2,1,0:T(4,128)S(1)} fusion(bf16[24,128,4,128]{1,3,2,0:T(8,128)(2,1)} %bitcast.217, f32[24,4,4,128]{3,2,1,0:T(4,128)S(1)} %get-tuple-element.48, f32[24,4,4]{2,1,0:T(4,128)S(1)} %broadcast_select_fusion.3, pred[24,128]{1,0:T(8,128)(4,1)S(1)} %iota_compare_fusion), kind=kOutput, calls=%fused_computation.53 | convolution fusion | flops 75595776 | bytes 3543552 | tf_op jit(solution)/shard_map/ikgt,itkd->ikgd/dot_general | solution.py:139
  238.9 0.7 convolution_add_fusion
  239.7 1.6 copy.197
  241.4 9.3 %all_gather.29 = f32[4,128,16]{1,2,0:T(8,128)S(1)} all-gather(f32[1,128,16]{1,2,0:T(8,128)S(1)} %bitcast.229), channel_id=1, replica_groups=mesh['grp'=4,'kv_0'=4,'kv_1'=4,'tp'=2] {'kv_0'}, dimensions={0}, use_global_device_ids=true | all-gather | bytes 40960 | tf_op jit(solution)/shard_map/all_gather | solution.py:27
  251.4 38.9 %all-gather.5.cloned.1.call-done = f32[4,128,16,128]{3,2,1,0:T(8,128)} async-done(((f32[1,128,16,128]{3,2,1,0:T(8,128)}), f32[4,128,16,128]{3,2,1,0:T(8,128)}) %all-gather.5.cloned.1.call-update) | async-done | bytes 4194320 | tf_op jit(solution)/shard_map/all_gather | solution.py:27
  290.2 4.8 fusion.3
  295.1 1.3 copy.211
  296.5 0.4 fusion.16
  297.0 0.2 convolution_add_fusion.1
  297.2 9.0 %all-gather = f32[512,16]{0,1:T(8,128)S(1)} all-gather(f32[128,16]{0,1:T(8,128)S(1)} %convolution_add_fusion.1), channel_id=2, replica_groups=mesh['grp'=4,'kv_0'=4,'kv_1'=4,'tp'=2] {'kv_0'}, dimensions={0}, use_global_device_ids=true | all-gather | bytes 40960 | tf_op jit(solution)/shard_map/all_gather | solution.py:27
  306.2 10.8 %all_gather.34 = f32[4,128,16]{1,2,0:T(8,128)S(1)} all-gather(f32[1,128,16]{1,2,0:T(8,128)S(1)} %get-tuple-element.22), channel_id=1, replica_groups=mesh['grp'=4,'kv_0'=4,'kv_1'=4,'tp'=2] {'kv_1'}, dimensions={0}, use_global_device_ids=true | all-gather | bytes 40960 | tf_op jit(solution)/shard_map/all_gather | solution.py:27
  317.0 10.6 %all_gather.31 = f32[4,128,16]{1,2,0:T(8,128)S(1)} all-gather(f32[1,128,16]{1,2,0:T(8,128)S(1)} %get-tuple-element.23), channel_id=1, replica_groups=mesh['grp'=4,'kv_0'=4,'kv_1'=4,'tp'=2] {'kv_1'}, dimensions={0}, use_global_device_ids=true | all-gather | bytes 40960 | tf_op jit(solution)/shard_map/all_gather | solution.py:27
  327.7 16.7 %all-gather.7.cloned.1.call-done = f32[4,128,16,128]{3,2,1,0:T(8,128)} async-done(((f32[1,128,16,128]{3,2,1,0:T(8,128)}), f32[4,128,16,128]{3,2,1,0:T(8,128)}) %all-gather.7.cloned.1.call-update) | async-done | bytes 4194320 | tf_op jit(solution)/shard_map/all_gather | solution.py:27
  344.3 3.9 fusion.78
  348.2 1.6 copy.227
  349.8 1.4 copy.229
  351.2 1.6 copy.228
  352.8 1.5 copy.230
  354.4 1.8 add_convert_fusion.1
  356.2 0.7 copy.213
  356.9 1.3 copy.214
  358.3 114.5 %all-gather.9.cloned.1.call-done = bf16[32,128,4096]{2,1,0:T(8,128)(2,1)} async-done(((bf16[1,128,4096]{2,1,0:T(8,128)(2,1)}), bf16[32,128,4096]{2,1,0:T(8,128)(2,1)}) %all-gather.9.cloned.1.call-update) | async-done | bytes 33554448 | tf_op jit(solution)/shard_map/all_gather | solution.py:21
  472.8 11.4 %reduce_sum.100 = bf16[128,4096]{1,0:T(8,128)(2,1)S(1)} reduce(bf16[32,128,4096]{2,1,0:T(8,128)(2,1)} %all-gather.9.cloned.1.call-done, bf16[]{:T(256)} %constant.131.clone.1), dimensions={0}, to_apply=%region_13.15 | reduce | flops 16252928 | bytes 34603008 | tf_op jit(solution)/shard_map/reduce_sum | solution.py:22
  484.2 0.7 copy.225
  484.9 0.6 multiply_reduce_fusion
  485.5 3.3 convolution_multiply_fusion.1
  488.7 6.1 %convolution_convert_fusion = bf16[128,4096]{1,0:T(8,128)(2,1)S(1)} fusion(bf16[448,4096]{1,0:T(8,128)(2,1)} %param.26, bf16[4096,448]{0,1:T(8,128)(2,1)} %param.25, f32[4096]{0:T(1024)S(1)} %copy-done.6, bf16[128,4096]{0,1:T(8,128)(2,1)S(1)} %copy.225, f32[128,448]{0,1:T(8,128)S(1)} %convolution_multiply_fusion.1, f32[128]{0:T(128)S(1)} %add_rsqrt_fusion), kind=kOutput, calls=%fused_computation.7 | convolution fusion | flops 942022656 | bytes 9683456 | tf_op jit(solution)/shard_map/dot_general | solution.py:219
  494.8 1.2 reshape.681
  496.0 5.3 all-to-all-start.2
  501.3 4.7 fusion.92
  506.1 12.1 %all-to-all-done.2 = bf16[32,4,4096]{2,1,0:T(4,128)(2,1)} async-done(((bf16[32,4,4096]{2,1,0:T(4,128)(2,1)}), bf16[32,4,4096]{2,1,0:T(4,128)(2,1)}, u32[]{:S(2)}, u32[]{:S(2)}) %all-to-all-start.2) | async-done | bytes 1048608 | tf_op jit(solution)/shard_map/all_to_all | solution.py:41
  518.3 1.7 convert_reduce_fusion
  519.9 2.0 copy.216
  521.9 3.2 add_convert_fusion
  525.1 2.2 copy.217
  (91 shorter events, 4.1 us)
Async XLA Ops:
  7.2 95.8 %copy-start = (bf16[256,2048]{1,0:T(8,128)(2,1)S(1)}, bf16[256,2048]{1,0:T(8,128)(2,1)}, u32[]{:S(2)}) copy-start(bf16[256,2048]{1,0:T(8,128)(2,1)} %param.22) | copy-start | bytes 3145732
  20.1 68.0 %all-to-all-start = ((bf16[16,2,128,512]{3,2,1,0:T(8,128)(2,1)}), bf16[16,2,128,512]{3,2,1,0:T(8,128)(2,1)}, u32[]{:S(2)}, u32[]{:S(2)}) async-start(bf16[16,2,128,512]{3,2,1,0:T(8,128)(2,1)} %broadcast_select_fusion.2), calls=%async_computation | async-start | bytes 8388608 | tf_op jit(solution)/shard_map/all_to_all | solution.py:89
  97.8 5.3 copy-start.5
  97.8 5.3 copy-start.7
  97.8 6.7 %copy-start.8 = (s32[1,16]{1,0:T(1,128)S(1)}, s32[1,16]{1,0:T(1,128)}, u32[]{:S(2)}) copy-start(s32[1,16]{1,0:T(1,128)} %param.33) | copy-start | bytes 196
  97.8 6.7 %copy-start.9 = (s32[1,8]{1,0:T(1,128)S(1)}, s32[1,8]{1,0:T(1,128)}, u32[]{:S(2)}) copy-start(s32[1,8]{1,0:T(1,128)} %param.29) | copy-start | bytes 100
  97.8 7.1 %copy-start.4 = (bf16[128,2,512]{2,1,0:T(2,128)(2,1)S(1)}, bf16[128,2,512]{2,1,0:T(2,128)(2,1)}, u32[]{:S(2)}) copy-start(bf16[128,2,512]{2,1,0:T(2,128)(2,1)} %param.35) | copy-start | bytes 786436
  97.8 107.8 %all-to-all-start.1 = ((bf16[16,2,128,512]{3,2,1,0:T(8,128)(2,1)}), bf16[16,2,128,512]{3,2,1,0:T(8,128)(2,1)}, u32[]{:S(2)}, u32[]{:S(2)}) async-start(bf16[16,2,128,512]{3,2,1,0:T(8,128)(2,1)} %broadcast_select_fusion.1), calls=%async_computation.1 | async-start | bytes 8388608 | tf_op jit(solution)/shard_map/all_to_all | solution.py:105
  103.0 2.3 copy-start.10
  103.0 2.3 copy-start.11
  103.0 98.0 %all-reduce.2.cloned.1.call-start = ((), (), s32[]{:S(2)}) async-start(), calls=%async_computation.3 | async-start | bytes 2097152 | tf_op jit(solution)/shard_map/psum | solution.py:180
  104.4 185.8 %all-gather.5.cloned.1.call-start = ((), (), s32[]{:S(2)}) async-start(), calls=%async_computation.4 | async-start | bytes 5242880 | tf_op jit(solution)/shard_map/all_gather | solution.py:27
  210.6 2.9 copy-start.2
  241.3 103.0 %all-gather.7.cloned.1.call-start = ((), (), s32[]{:S(2)}) async-start(), calls=%async_computation.5 | async-start | bytes 5242880 | tf_op jit(solution)/shard_map/all_gather | solution.py:27
  250.8 44.4 %copy-start.3 = (bf16[16,8,4096]{2,1,0:T(8,128)(2,1)S(1)}, bf16[16,8,4096]{2,1,0:T(8,128)(2,1)}, u32[]{:S(2)}) copy-start(bf16[16,8,4096]{2,1,0:T(8,128)(2,1)} %param.23) | copy-start | bytes 3145732
  295.1 177.8 %all-gather.9.cloned.1.call-start = ((), (), s32[]{:S(2)}) async-start(), calls=%async_computation.6 | async-start | bytes 34603008 | tf_op jit(solution)/shard_map/all_gather | solution.py:21
  358.3 127.2 %copy-start.6 = (f32[4096]{0:T(1024)S(1)}, f32[4096]{0:T(1024)}, u32[]{:S(2)}) copy-start(f32[4096]{0:T(1024)} %param.21) | copy-start | bytes 49156
  496.0 22.2 %all-to-all-start.2 = ((bf16[32,4,4096]{2,1,0:T(4,128)(2,1)}), bf16[32,4,4096]{2,1,0:T(4,128)(2,1)}, u32[]{:S(2)}, u32[]{:S(2)}) async-start(bf16[32,4,4096]{2,1,0:T(4,128)(2,1)} %reshape.681), calls=%async_computation.2 | async-start | bytes 2097152 | tf_op jit(solution)/shard_map/all_to_all | solution.py:41
  519.9 7.4 %copy-start.1 = (bf16[256,2048]{1,0:T(8,128)(2,1)S(1)}, bf16[256,2048]{1,0:T(8,128)(2,1)}, u32[]{:S(2)}) copy-start(bf16[256,2048]{1,0:T(8,128)(2,1)} %param.22) | copy-start | bytes 3145732
Sparse Core Ops, SparseCore 0:
  107.0 93.8 all-reduce.1
  241.4 48.7 all-gather.4
  295.2 49.0 all-gather.6
  358.4 114.3 all-gather.8
